TPU v7x, 32 devices: a whole 2x2x4 slice. The times are simulated.
32 devices in a mesh: rows: 8 (over z, y), dp: 4 (over x, core).
Axes of the slice: x: 2, y: 2, z: 4, core: 2. Of those that a mesh axis runs over, the one named last changes fastest.
Arguments:
- weights: float32 [6144, 4096], P(('rows', 'dp'))
- moment: float32 [6144, 4096], P(('rows', 'dp'))
- second: float32 [6144, 4096], P(('rows', 'dp')), may hold values from 0.01 to 1
- tile_rows: bfloat16 [2048, 4096], P(('rows', 'dp')), may hold values from -6 to 6
- row_index: int32 [2048], P(('rows', 'dp')), may hold values from 0 to 191
- bucket_count: int32 [1024], P(('rows', 'dp')), may hold values from 1 to 2, as said below
Outputs:
- new_weights: float32 [6144, 4096], P(('rows', 'dp'))
- new_moment: float32 [6144, 4096], P(('rows', 'dp'))
- new_second: float32 [6144, 4096], P(('rows', 'dp'))
Inputs may be any that keep to these rules, and one draw needn't show every extreme that they name: `bucket_count`: at least one slot of every sender and owner is live; in every draw some owner receives 2 live slots from every sender. `row_index`: rows may repeat within and across senders.
All inputs are finite; a program needn't handle non-finite values.
Results may differ from a plain program's by a relative error of at most 0.0003.
Values may be sent and summed in bfloat16 or wider, within the bound.
No kernel may reach another device: no remote copies, remote signals or barrier semaphores. Data moves between devices by JAX's collectives and lax.ppermute only.
A program may use at most 64 MiB of HBM per device.

v0:
```python
import jax
import jax.numpy as jnp
from jax import lax
from jax.sharding import PartitionSpec as P

beta_one = 0.9
beta_two = 0.999
epsilon = 1e-06
decay = 0.01
rate = 0.1


def local(weights, moment, second, tile_rows, row_index, bucket_count):
    owners = lax.axis_size(("rows", "dp"))
    rows_here = weights.shape[0]
    slot_total = row_index.shape[0]
    capacity = slot_total // owners
    is_live = lax.broadcasted_iota(jnp.int32, (owners, capacity), 1) < bucket_count[:, None]
    target = jnp.where(is_live.reshape(-1), row_index, -1)
    weight_part = jnp.sum(weights * weights)
    arrived, landing = (
        lax.all_to_all(tile_rows, ("rows", "dp"), split_axis=0, concat_axis=0, tiled=True),
        lax.all_to_all(target, ("rows", "dp"), split_axis=0, concat_axis=0, tiled=True),
    )
    picker = (
        landing[None, :] == lax.broadcasted_iota(jnp.int32, (rows_here, slot_total), 0)
    ).astype(jnp.bfloat16)
    gradient = jnp.dot(picker, arrived, preferred_element_type=jnp.float32)
    new_moment = beta_one * moment + (1.0 - beta_one) * gradient
    new_second = beta_two * second + (1.0 - beta_two) * gradient * gradient
    update = new_moment / (jnp.sqrt(new_second) + epsilon) + decay * weights
    update_part = jnp.sum(update * update)
    weight_sq, update_sq = lax.psum((weight_part, update_part), ("rows", "dp"))
    trust_ratio = jnp.sqrt(weight_sq) / jnp.sqrt(update_sq + 1e-06)
    new_weights = weights - rate * trust_ratio * update
    return (new_weights, new_moment, new_second)


def solution(mesh):
    placed = (
        P(("rows", "dp"), None),
        P(("rows", "dp"), None),
        P(("rows", "dp"), None),
        P(("rows", "dp"), None),
        P(("rows", "dp")),
        P(("rows", "dp")),
    )
    return jax.shard_map(
        local,
        mesh=mesh,
        in_specs=placed,
        out_specs=(P(("rows", "dp"), None), P(("rows", "dp"), None), P(("rows", "dp"), None)),
        check_vma=False,
    )
```

profile of v0, /device:TPU:0, one launch (start us, length us, event | category | flops | bytes accessed | tf_op | source)
XLA Modules:
  0.0 91.9 jit_solution(8254244321637544853)
XLA Ops:
  0.6 0.0 copy-start
  0.6 0.9 iota_compare_fusion.2
  1.5 0.1 lt.14
  1.6 0.7 broadcast_select_fusion
  2.3 0.7 all_to_all.14
  3.0 7.3 %all-to-all-start = ((s32[32,2,1]{1,2,0:T(1,128)}), s32[32,2,1]{1,2,0:T(1,128)S(1)}, u32[]{:S(2)}, u32[]{:S(2)}) async-start(s32[32,2,1]{1,2,0:T(1,128)} %bitcast), calls=%async_computation | async-start | bytes 32768 | tf_op jit(solution)/shard_map/all_to_all | solution.py:23
  10.3 2.2 %all_to_all.16 = bf16[32,2,4096]{2,1,0:T(2,128)(2,1)} reshape(bf16[64,4096]{1,0:T(8,128)(2,1)} %param.9) | data formatting | bytes 1048576 | tf_op jit(solution)/shard_map/all_to_all | solution.py:22
  12.5 4.9 %all-to-all-done = s32[32,2,1]{1,2,0:T(1,128)S(1)} async-done(((s32[32,2,1]{1,2,0:T(1,128)}), s32[32,2,1]{1,2,0:T(1,128)S(1)}, u32[]{:S(2)}, u32[]{:S(2)}) %all-to-all-start) | async-done | bytes 288 | tf_op jit(solution)/shard_map/all_to_all | solution.py:23
  17.4 3.3 %all-to-all-start.1 = ((bf16[32,2,4096]{2,1,0:T(2,128)(2,1)}), bf16[32,2,4096]{2,1,0:T(2,128)(2,1)}, u32[]{:S(2)}, u32[]{:S(2)}) async-start(bf16[32,2,4096]{2,1,0:T(2,128)(2,1)} %all_to_all.16), calls=%async_computation.1 | async-start | bytes 1048576 | tf_op jit(solution)/shard_map/all_to_all | solution.py:22
  20.8 0.5 broadcast.7
  21.3 0.7 reduce.3
  22.0 0.1 eq.10
  22.1 14.3 %all-to-all-done.1 = bf16[32,2,4096]{2,1,0:T(2,128)(2,1)} async-done(((bf16[32,2,4096]{2,1,0:T(2,128)(2,1)}), bf16[32,2,4096]{2,1,0:T(2,128)(2,1)}, u32[]{:S(2)}, u32[]{:S(2)}) %all-to-all-start.1) | async-done | bytes 524320 | tf_op jit(solution)/shard_map/all_to_all | solution.py:22
  36.4 2.0 %all_to_all.18 = bf16[64,4096]{1,0:T(8,128)(2,1)} reshape(bf16[32,2,4096]{2,1,0:T(2,128)(2,1)} %all-to-all-done.1) | data formatting | bytes 1048576 | tf_op jit(solution)/shard_map/all_to_all | solution.py:22
  38.4 0.0 copy-done
  38.4 7.0 %multiply_reduce_fusion = (f32[]{:T(128)}, f32[]{:T(128)}, f32[192,4096]{1,0:T(8,128)}, f32[192,4096]{1,0:T(8,128)}) fusion(f32[192,4096]{1,0:T(8,128)S(1)} %copy-done, f32[192,4096]{1,0:T(8,128)} %param.8, f32[192,4096]{1,0:T(8,128)} %param.7, bf16[64,4096]{1,0:T(8,128)(2,1)} %all_to_all.18, s32[64]{0:T(128)S(1)} %eq.10), kind=kOutput, calls=%fused_computation.3 | convolution fusion | flops 112472064 | bytes 16253192 | tf_op jit(solution)/shard_map/dot_general | solution.py:28
  45.4 39.1 %all-reduce = (f32[]{:T(128)}, f32[]{:T(128)}) all-reduce(f32[]{:T(128)} %get-tuple-element.4, f32[]{:T(128)} %get-tuple-element.3), channel_id=1, replica_groups=mesh['rows'=8,'dp'=4] {'rows','dp'}, use_global_device_ids=true, to_apply=%region_1.2 | all-reduce | flops 2 | bytes 16 | tf_op jit(solution)/shard_map/psum | solution.py:33
  85.9 6.0 %multiply_subtract_fusion = f32[192,4096]{1,0:T(8,128)} fusion(f32[192,4096]{1,0:T(8,128)S(1)} %copy-done, f32[]{:T(128)S(6)} %mul.61, f32[192,4096]{1,0:T(8,128)} %get-tuple-element.8, f32[192,4096]{1,0:T(8,128)} %get-tuple-element.7), kind=kLoop, calls=%fused_computation.2 | loop fusion | flops 4718592 | bytes 12582916 | tf_op jit(solution)/shard_map/sub | solution.py:35
Async XLA Ops:
  0.6 37.8 %copy-start = (f32[192,4096]{1,0:T(8,128)S(1)}, f32[192,4096]{1,0:T(8,128)}, u32[]{:S(2)}) copy-start(f32[192,4096]{1,0:T(8,128)} %param.6) | copy-start | bytes 9437188
  3.0 14.4 %all-to-all-start = ((s32[32,2,1]{1,2,0:T(1,128)}), s32[32,2,1]{1,2,0:T(1,128)S(1)}, u32[]{:S(2)}, u32[]{:S(2)}) async-start(s32[32,2,1]{1,2,0:T(1,128)} %bitcast), calls=%async_computation | async-start | bytes 32768 | tf_op jit(solution)/shard_map/all_to_all | solution.py:23
  17.4 18.9 %all-to-all-start.1 = ((bf16[32,2,4096]{2,1,0:T(2,128)(2,1)}), bf16[32,2,4096]{2,1,0:T(2,128)(2,1)}, u32[]{:S(2)}, u32[]{:S(2)}) async-start(bf16[32,2,4096]{2,1,0:T(2,128)(2,1)} %all_to_all.16), calls=%async_computation.1 | async-start | bytes 1048576 | tf_op jit(solution)/shard_map/all_to_all | solution.py:22
where the time goes:
time: 92.4 us; the launch traced here: 91.9 us
  blocking collectives  39.1 us (42%)
  waiting for transfers between devices  19.2 us (21%)
  starting transfers between devices  10.7 us (12%)
  other arithmetic  8.18 us (9%)
  matrix products  7.01 us (8%)
  local copies, waits for them, and re-layouts  5.65 us (6%)
  between operations  2.04 us (2%)
    psum x1, blocking collectives, local(): weight_sq, update_sq = lax.psum((weight_part, update_part), ('rows', 'dp'))  39.1 us
    all_to_all x1, waiting for transfers between devices, local(): lax.all_to_all(tile_rows, ('rows', 'dp'), split_axis=0, concat_axis=0, ti...  14.3 us
    all_to_all x1, starting transfers between devices, local(): lax.all_to_all(target, ('rows', 'dp'), split_axis=0, concat_axis=0, tiled...  7.33 us
    dot_general x1, matrix products, local(): gradient = jnp.dot(picker, arrived, preferred_element_type=jnp.float32)  7.01 us
    sub x1, other arithmetic, local(): new_weights = weights - rate * trust_ratio * update  5.96 us
    all_to_all x1, waiting for transfers between devices, local(): lax.all_to_all(target, ('rows', 'dp'), split_axis=0, concat_axis=0, tiled...  4.93 us
    all_to_all x2, local copies, waits for them, and re-layouts, local(): lax.all_to_all(tile_rows, ('rows', 'dp'), split_axis=0, concat_axis=0, ti...  4.2 us
    all_to_all x1, starting transfers between devices, local(): lax.all_to_all(tile_rows, ('rows', 'dp'), split_axis=0, concat_axis=0, ti...  3.33 us
  transfers between devices with their start and end apart: 2, of which 2 were waited for; matrix products, arithmetic and copies ran while one was open for 1% of the time, Pallas kernels for 0%

commit v1 on v0

v1 whole, which is shorter than its diff:
```python
import jax
import jax.numpy as jnp
from jax import lax
from jax.sharding import PartitionSpec as P

beta_one = 0.9
beta_two = 0.999
epsilon = 1e-06
decay = 0.01
rate = 0.1
LANES = 128
AXES = ("rows", "dp")


def local(weights, moment, second, tile_rows, row_index, bucket_count):
    owners = lax.axis_size(AXES)
    rows_here, width = weights.shape
    slot_total = row_index.shape[0]
    capacity = slot_total // owners
    is_live = lax.broadcasted_iota(jnp.int32, (owners, capacity), 1) < bucket_count[:, None]
    target = jnp.where(is_live, row_index.reshape(owners, capacity), -1)[:, :, None]
    lane = lax.broadcasted_iota(jnp.int32, (owners, capacity, LANES), 2)
    digits = jnp.where(lane == 0, target >> 7, target & 127).astype(jnp.bfloat16)
    packed = jnp.concatenate([tile_rows.reshape(owners, capacity, width), digits], axis=2)
    arrived = lax.all_to_all(packed, AXES, split_axis=0, concat_axis=0, tiled=True)
    arrived = arrived.reshape(slot_total, width + LANES)
    landing = arrived[:, width].astype(jnp.int32) * 128 + arrived[:, width + 1].astype(jnp.int32)
    picker = (
        landing[None, :] == lax.broadcasted_iota(jnp.int32, (rows_here, slot_total), 0)
    ).astype(jnp.bfloat16)
    gradient = jnp.dot(picker, arrived[:, :width], preferred_element_type=jnp.float32)
    new_moment = beta_one * moment + (1.0 - beta_one) * gradient
    new_second = beta_two * second + (1.0 - beta_two) * gradient * gradient
    update = new_moment / (jnp.sqrt(new_second) + epsilon) + decay * weights
    parts = jnp.stack([jnp.sum(weights * weights), jnp.sum(update * update)])
    told = jnp.broadcast_to(parts[None, :, None], (owners, 2, LANES))
    heard = lax.all_to_all(told, AXES, split_axis=0, concat_axis=0, tiled=True)
    sums = jnp.sum(heard[:, :, 0], axis=0)
    trust_ratio = jnp.sqrt(sums[0]) / jnp.sqrt(sums[1] + 1e-06)
    new_weights = weights - rate * trust_ratio * update
    return (new_weights, new_moment, new_second)


def solution(mesh):
    placed = (P(AXES, None),) * 4 + (P(AXES),) * 2
    return jax.shard_map(
        local, mesh=mesh, in_specs=placed, out_specs=(P(AXES, None),) * 3, check_vma=False
    )
```

time: 92.4 us -> 55 us (0.60)
  waiting for transfers between devices: 19.2 us -> 0 us
  starting transfers between devices: 10.7 us -> 0 us
  blocking collectives: 39.1 us -> 33.2 us
  matrix products: 7.01 us -> 5.39 us
    psum x1 -> x0, blocking collectives: 39.1 us -> none  [local(): weight_sq, update_sq = lax.psum((weight_part, update_part), ('rows', 'dp'))]
    all_to_all x0 -> x2, blocking collectives: none -> 33.2 us  [the longest x1 23.1 us: local(): lax.all_to_all(packed, AXES, split_axis=0, concat_axis=0, tiled=True)]
    all_to_all x2 -> x0, waiting for transfers between devices: 19.2 us -> none  [the longest x1 14.3 us: local(): lax.all_to_all(tile_rows, ('rows', 'dp'), split_axis=0, concat_axis=0, ti...]
    all_to_all x2 -> x0, starting transfers between devices: 10.7 us -> none  [the longest x1 7.33 us: local(): lax.all_to_all(target, ('rows', 'dp'), split_axis=0, concat_axis=0, tiled...]
    all_to_all x4 -> x0, local copies, waits for them, and re-layouts: 5.43 us -> none  [the longest x2 4.2 us: local(): lax.all_to_all(tile_rows, ('rows', 'dp'), split_axis=0, concat_axis=0, ti...]
    reshape x0 -> x3, local copies, waits for them, and re-layouts: none -> 5.15 us  [the longest x1 2.2 us: local(): tile_rows.reshape(owners, capacity, width)]
    sub x1, other arithmetic: 5.96 us -> 3.1 us  [local(): new_weights = weights - rate * trust_ratio * update]
    dot_general x1, matrix products: 7.01 us -> 5.39 us  [local(): jnp.dot(picker, arrived[:, :width], preferred_element_type=jnp.float32)]
  transfers between devices with their start and end apart: 2 -> 0, of which waited for: 2 -> 0; matrix products, arithmetic and copies ran while one was open for 1% -> 0% of each run, Pallas kernels for 0% -> 0%
where the time goes in v1:
time: 55 us; the launch traced here: 54.7 us
  blocking collectives  33.2 us (60%)
  other arithmetic  8.09 us (15%)
  local copies, waits for them, and re-layouts  5.84 us (11%)
  matrix products  5.39 us (10%)
  between operations  2.11 us (4%)
    all_to_all x1, blocking collectives, local(): lax.all_to_all(packed, AXES, split_axis=0, concat_axis=0, tiled=True)  23.1 us
    all_to_all x1, blocking collectives, local(): heard = lax.all_to_all(told, AXES, split_axis=0, concat_axis=0, tiled=True)  10.1 us
    dot_general x1, matrix products, local(): jnp.dot(picker, arrived[:, :width], preferred_element_type=jnp.float32)  5.39 us
    sub x1, other arithmetic, local(): new_weights = weights - rate * trust_ratio * update  3.1 us
    reshape x1, local copies, waits for them, and re-layouts, local(): tile_rows.reshape(owners, capacity, width)  2.2 us
    reshape x1, local copies, waits for them, and re-layouts, local(): arrived = arrived.reshape(slot_total, width + LANES)  2.05 us
    concatenate x1, other arithmetic, local(): jnp.concatenate([tile_rows.reshape(owners, capacity, width), digits], axi...  1.56 us
    another operation x1, other arithmetic, local(): parts = jnp.stack([jnp.sum(weights * weights), jnp.sum(update * update)])  1.45 us

profile of v1, /device:TPU:0, one launch (start us, length us, event | category | flops | bytes accessed | tf_op | source)
XLA Modules:
  0.0 54.7 jit_solution(9288025314276561281)
XLA Ops:
  0.6 0.0 copy-start
  0.7 0.9 %reshape.87 = s32[32,2]{1,0:T(8,128)S(1)} reshape(s32[64]{0:T(128)} %param.10) | data formatting | bytes 512 | tf_op jit(solution)/shard_map/reshape | solution.py:21
  1.6 2.2 %reshape.86 = bf16[32,2,4096]{2,1,0:T(2,128)(2,1)} reshape(bf16[64,4096]{1,0:T(8,128)(2,1)} %param.9) | data formatting | bytes 1048576 | tf_op jit(solution)/shard_map/reshape | solution.py:24
  3.8 0.7 %fusion.6 = (s32[32,2]{1,0:T(8,128)S(1)}, s32[32,2]{1,0:T(8,128)S(1)}) fusion(s32[32,2]{1,0:T(8,128)S(1)} %reshape.87, s32[32]{0:T(128)} %param.11), kind=kLoop, calls=%fused_computation.18 | loop fusion | flops 256 | bytes 896 | tf_op jit(solution)/shard_map/shift_right_arithmetic | solution.py:23
  4.5 0.1 select_convert_fusion
  4.6 1.6 %pad_maximum_fusion = bf16[32,2,4224]{2,1,0:T(2,128)(2,1)S(1)} fusion(bf16[32,2,128]{2,1,0:T(2,128)(2,1)S(1)} %select_convert_fusion, bf16[32,2,4096]{2,1,0:T(2,128)(2,1)} %reshape.86), kind=kLoop, calls=%fused_computation.7 | loop fusion | flops 1081344 | bytes 1081344 | tf_op jit(solution)/shard_map/concatenate | solution.py:24
  6.2 23.1 %all_to_all.10 = bf16[32,2,4224]{2,1,0:T(2,128)(2,1)} all-to-all(bf16[32,2,4224]{2,1,0:T(2,128)(2,1)S(1)} %pad_maximum_fusion), channel_id=1, replica_groups=mesh['rows'=8,'dp'=4] {'rows','dp'}, dimensions={0} | all-to-all | bytes 1081344 | tf_op jit(solution)/shard_map/all_to_all | solution.py:25
  29.3 2.0 %reshape.88 = bf16[64,4224]{1,0:T(8,128)(2,1)} reshape(bf16[32,2,4224]{2,1,0:T(2,128)(2,1)} %all_to_all.10) | data formatting | bytes 1081344 | tf_op jit(solution)/shard_map/reshape | solution.py:26
  31.4 1.0 %add_reduce_fusion = s32[64]{0:T(128)S(1)} fusion(bf16[64,4224]{1,0:T(8,128)(2,1)} %reshape.88), kind=kLoop, calls=%fused_computation.13 | loop fusion | flops 256 | bytes 512 | tf_op jit(solution)/shard_map/add | solution.py:27
  32.4 0.0 copy-done
  32.4 5.4 %multiply_reduce_fusion.1 = (f32[]{:T(128)}, f32[]{:T(128)}, f32[192,4096]{1,0:T(8,128)S(1)}, f32[192,4096]{1,0:T(8,128)S(1)}) fusion(f32[192,4096]{1,0:T(8,128)S(1)} %copy-done, f32[192,4096]{1,0:T(8,128)} %param.8, f32[192,4096]{1,0:T(8,128)} %param.7, bf16[64,4224]{1,0:T(8,128)(2,1)} %reshape.88, s32[64]{0:T(128)S(1)} %add_reduce_fusion), kind=kOutput, calls=%fused_computation.6 | convolution fusion | flops 112472064 | bytes 16253192 | tf_op jit(solution)/shard_map/dot_general | solution.py:31
  37.8 0.0 copy-start.1
  37.8 0.0 copy-start.2
  37.8 1.5 %pad_maximum_fusion.1 = f32[2]{0:T(128)S(1)} fusion(f32[1]{0:T(128)} %bitcast.1, f32[1]{0:T(128)} %bitcast), kind=kLoop, calls=%fused_computation.19 | loop fusion | flops 2 | bytes 16 | tf_op jit(solution)/shard_map/stack | solution.py:35
  39.2 0.1 broadcast_in_dim.32
  39.3 10.1 %all_to_all.11 = f32[32,2,128]{2,1,0:T(2,128)S(1)} all-to-all(f32[32,2,128]{2,1,0:T(2,128)S(1)} %broadcast_in_dim.32), channel_id=1, replica_groups=mesh['rows'=8,'dp'=4] {'rows','dp'}, dimensions={0} | all-to-all | bytes 65536 | tf_op jit(solution)/shard_map/all_to_all | solution.py:37
  49.4 0.1 slice_reduce_fusion
  49.5 0.6 %fusion.8 = (f32[1]{0:T(128)}, f32[1]{0:T(128)}) fusion(f32[2]{0:T(128)S(1)} %slice_reduce_fusion), kind=kLoop, calls=%fused_computation.21 | loop fusion | bytes 16 | tf_op jit(solution)/shard_map/slice | solution.py:39
  51.6 3.1 %multiply_subtract_fusion = f32[192,4096]{1,0:T(8,128)} fusion(f32[192,4096]{1,0:T(8,128)S(1)} %copy-done, f32[]{:T(128)} %bitcast.2, f32[192,4096]{1,0:T(8,128)S(1)} %get-tuple-element.6, f32[192,4096]{1,0:T(8,128)S(1)} %get-tuple-element.5), kind=kLoop, calls=%fused_computation.2 | loop fusion | flops 4718592 | bytes 12582916 | tf_op jit(solution)/shard_map/sub | solution.py:40
  54.7 0.0 copy-done.1
  54.7 0.0 copy-done.2
  (1 shorter events, 0.0 us)
Async XLA Ops:
  0.6 31.7 %copy-start = (f32[192,4096]{1,0:T(8,128)S(1)}, f32[192,4096]{1,0:T(8,128)}, u32[]{:S(2)}) copy-start(f32[192,4096]{1,0:T(8,128)} %param.6) | copy-start | bytes 9437188
  37.8 16.9 %copy-start.1 = (f32[192,4096]{1,0:T(8,128)}, f32[192,4096]{1,0:T(8,128)S(1)}, u32[]{:S(2)}) copy-start(f32[192,4096]{1,0:T(8,128)S(1)} %get-tuple-element.5) | copy-start | bytes 9437188
  37.8 16.9 %copy-start.2 = (f32[192,4096]{1,0:T(8,128)}, f32[192,4096]{1,0:T(8,128)S(1)}, u32[]{:S(2)}) copy-start(f32[192,4096]{1,0:T(8,128)S(1)} %get-tuple-element.6) | copy-start | bytes 9437188

commit v2 on v1

v2 whole, which is shorter than its diff:
```python
import functools
import math

import jax
import jax.numpy as jnp
from jax import lax
from jax.experimental import pallas as pl
from jax.experimental.pallas import tpu as pltpu
from jax.sharding import PartitionSpec as P

beta_one = 0.9
beta_two = 0.999
epsilon = 1e-06
decay = 0.01
rate = 0.1
LANES = 128
AXES = ("rows", "dp")
MIB = 1 << 20

VMEM = pl.BlockSpec(memory_space=pltpu.VMEM)
SMEM = pl.BlockSpec(memory_space=pltpu.SMEM)
ANY = pl.BlockSpec(memory_space=pl.ANY)


def cost(flops):
    return pl.CostEstimate(flops=flops, bytes_accessed=0, transcendentals=0)


def start(token_ref):
    token_ref[...] = jnp.zeros_like(token_ref)


def address(token_ref, index_ref, count_ref, out_ref):
    del token_ref
    owners, capacity, lanes = out_ref.shape
    slots = owners * capacity
    slot = lax.broadcasted_iota(jnp.int32, (slots, slots), 0)
    across = lax.broadcasted_iota(jnp.int32, (slots, slots), 1)
    index = jnp.broadcast_to(index_ref[...].reshape(1, slots), (slots, slots))
    index = jnp.sum(jnp.where(slot == across, index, 0), axis=1, keepdims=True)
    owner = lax.broadcasted_iota(jnp.int32, (slots, owners), 0) // capacity
    across = lax.broadcasted_iota(jnp.int32, (slots, owners), 1)
    count = jnp.broadcast_to(count_ref[...].reshape(1, owners), (slots, owners))
    count = jnp.sum(jnp.where(owner == across, count, 0), axis=1, keepdims=True)
    place = lax.broadcasted_iota(jnp.int32, (slots, 1), 0) % capacity
    target = jnp.broadcast_to(jnp.where(place < count, index, -1), (slots, lanes))
    lane = lax.broadcasted_iota(jnp.int32, (slots, lanes), 1)
    digits = jnp.where(lane == 0, target >> 7, target & 127)
    digits = digits.astype(jnp.float32).astype(jnp.bfloat16)
    out_ref[...] = digits.reshape(owners, capacity, lanes)


def pack(digits_ref, tile_ref, out_ref):
    owners, capacity, padded = out_ref.shape
    width = padded - LANES
    out_ref[:, :, width:] = digits_ref[...]
    out_ref[:, :, :width] = tile_ref[...].reshape(owners, capacity, width)


def advance(block, tile, arrived_ref, weights_ref, moment_ref, second_ref,
            new_moment_hbm, new_second_hbm, update_ref, told_ref,
            new_moment_ref, new_second_ref, even_ref, odd_ref, sem):
    rows_here, width = weights_ref.shape
    owners, capacity, _ = arrived_ref.shape
    slots = owners * capacity
    blocks = width // block
    digits = arrived_ref[:, :, width:].reshape(slots, LANES).astype(jnp.float32)
    landing = (digits[:, 0:1] * 128.0 + digits[:, 1:2]).astype(jnp.int32)
    picker = (
        landing == lax.broadcasted_iota(jnp.int32, (slots, rows_here), 1)
    ).astype(jnp.float32).T.astype(jnp.bfloat16)

    def gather(j, gradient_ref):
        for k in range(0, block, tile):
            sent = arrived_ref[:, :, j * block + k:j * block + k + tile].reshape(slots, tile)
            gradient_ref[:, k:k + tile] = jnp.dot(picker, sent, preferred_element_type=jnp.float32)

    weight_sum = jnp.zeros((8, block), jnp.float32)
    update_sum = jnp.zeros((8, block), jnp.float32)
    stores = []
    gather(0, even_ref)
    for j in range(blocks):
        gradient_ref, next_ref = (even_ref, odd_ref) if j % 2 == 0 else (odd_ref, even_ref)
        if j + 1 < blocks:
            gather(j + 1, next_ref)
        cols = pl.ds(j * block, block)
        for r in range(0, rows_here, 8):
            rows = pl.ds(r, 8)
            gradient = gradient_ref[rows, :]
            weights = weights_ref[rows, cols]
            new_moment = beta_one * moment_ref[rows, cols] + (1.0 - beta_one) * gradient
            new_second = beta_two * second_ref[rows, cols] + (1.0 - beta_two) * gradient * gradient
            root = new_second * lax.rsqrt(new_second)
            update = new_moment / (root + epsilon) + decay * weights
            new_moment_ref[rows, cols] = new_moment
            new_second_ref[rows, cols] = new_second
            update_ref[rows, cols] = update
            weight_sum += weights * weights
            update_sum += update * update
        for k, (held, out) in enumerate(((new_moment_ref, new_moment_hbm), (new_second_ref, new_second_hbm))):
            stores.append(pltpu.make_async_copy(held.at[:, cols], out.at[:, cols], sem.at[k, j]))
            stores[-1].start()

    def narrow(x):
        x = jnp.sum(x, axis=0, keepdims=True)
        return sum(x[:, k:k + LANES] for k in range(0, block, LANES))

    both = jnp.concatenate([narrow(weight_sum), narrow(update_sum)], axis=0)
    told_ref[...] = jnp.broadcast_to(both[None], told_ref.shape)
    for store in stores:
        store.wait()


def apply(chunk, heard_ref, weights_ref, update_ref, out_ref, held_ref, sem):
    sums = jnp.sum(jnp.sum(heard_ref[...], axis=0), axis=1, keepdims=True)
    scale = rate * (jnp.sqrt(sums[0:1]) / jnp.sqrt(sums[1:2] + 1e-06))
    stores = []
    for k in range(weights_ref.shape[0] // chunk):
        rows = pl.ds(k * chunk, chunk)
        held_ref[rows, :] = weights_ref[rows, :] - scale * update_ref[rows, :]
        stores.append(pltpu.make_async_copy(held_ref.at[rows, :], out_ref.at[rows, :], sem.at[k]))
        stores[-1].start()
    for store in stores:
        store.wait()


def local(weights, moment, second, tile_rows, row_index, bucket_count):
    owners = lax.axis_size(AXES)
    rows_here, width = weights.shape
    slot_total = row_index.shape[0]
    capacity = slot_total // owners
    block = math.gcd(width, 512)
    tile = math.gcd(width, 256)
    chunk = 24
    table = jax.ShapeDtypeStruct((rows_here, width), jnp.float32)
    token = pl.pallas_call(
        start,
        out_shape=jax.ShapeDtypeStruct((8, LANES), jnp.float32),
        out_specs=VMEM,
        compiler_params=pltpu.CompilerParams(vmem_limit_bytes=MIB),
        cost_estimate=cost(10000000000),
        name="start",
    )()
    digits = pl.pallas_call(
        address,
        out_shape=jax.ShapeDtypeStruct((owners, capacity, LANES), jnp.bfloat16),
        in_specs=[VMEM] * 3,
        out_specs=VMEM,
        compiler_params=pltpu.CompilerParams(vmem_limit_bytes=4 * MIB),
        cost_estimate=cost(1000000),
        name="address",
    )(token, row_index, bucket_count)
    packed = pl.pallas_call(
        pack,
        out_shape=jax.ShapeDtypeStruct((owners, capacity, width + LANES), jnp.bfloat16),
        in_specs=[VMEM] * 2,
        out_specs=VMEM,
        compiler_params=pltpu.CompilerParams(vmem_limit_bytes=16 * MIB),
        cost_estimate=cost(10000000000),
        name="pack",
    )(digits, tile_rows)
    arrived = lax.all_to_all(packed, AXES, split_axis=0, concat_axis=0, tiled=True)
    new_moment, new_second, update, told = pl.pallas_call(
        functools.partial(advance, block, tile),
        out_shape=(table,) * 3 + (jax.ShapeDtypeStruct((owners, 2, LANES), jnp.float32),),
        in_specs=[VMEM] * 4,
        out_specs=(ANY, ANY, VMEM, VMEM),
        scratch_shapes=[
            pltpu.VMEM((rows_here, width), jnp.float32),
            pltpu.VMEM((rows_here, width), jnp.float32),
            pltpu.VMEM((rows_here, block), jnp.float32),
            pltpu.VMEM((rows_here, block), jnp.float32),
            pltpu.SemaphoreType.DMA((2, width // block)),
        ],
        compiler_params=pltpu.CompilerParams(vmem_limit_bytes=32 * MIB),
        cost_estimate=cost(100000000),
        name="advance",
    )(arrived, weights, moment, second)
    heard = lax.all_to_all(told, AXES, split_axis=0, concat_axis=0, tiled=True)
    new_weights = pl.pallas_call(
        functools.partial(apply, chunk),
        out_shape=table,
        in_specs=[VMEM] * 3,
        out_specs=ANY,
        scratch_shapes=[
            pltpu.VMEM((rows_here, width), jnp.float32),
            pltpu.SemaphoreType.DMA((rows_here // chunk,)),
        ],
        compiler_params=pltpu.CompilerParams(vmem_limit_bytes=24 * MIB),
        cost_estimate=cost(1000000),
        name="apply",
    )(heard, weights, update)
    return (new_weights, new_moment, new_second)


def solution(mesh):
    placed = (P(AXES, None),) * 4 + (P(AXES),) * 2
    return jax.shard_map(
        local, mesh=mesh, in_specs=placed, out_specs=(P(AXES, None),) * 3, check_vma=False
    )
```

time: 55 us -> 40.6 us (0.74)
  other arithmetic: 8.09 us -> 0 us
  Pallas kernels: 0 us -> 5.67 us
  matrix products: 5.39 us -> 0 us
  local copies, waits for them, and re-layouts: 5.84 us -> 0.92 us
  between operations: 2.11 us -> 0.69 us
    pallas_call x0 -> x5, Pallas kernels: none -> 5.67 us  [the longest x1 3.53 us: local(): pl.pallas_call(functools.partial(advance, block, tile), out_shape=(table,...]
    dot_general x1 -> x0, matrix products: 5.39 us -> none  [local(): jnp.dot(picker, arrived[:, :width], preferred_element_type=jnp.float32)]
    reshape x3 -> x0, local copies, waits for them, and re-layouts: 5.15 us -> none  [the longest x1 2.2 us: local(): tile_rows.reshape(owners, capacity, width)]
    sub x1 -> x0, other arithmetic: 3.1 us -> none  [local(): new_weights = weights - rate * trust_ratio * update]
    concatenate x1 -> x0, other arithmetic: 1.56 us -> none  [local(): jnp.concatenate([tile_rows.reshape(owners, capacity, width), digits], axi...]
    another operation x1 -> x0, other arithmetic: 1.45 us -> none  [local(): parts = jnp.stack([jnp.sum(weights * weights), jnp.sum(update * update)])]
    add x1 -> x0, other arithmetic: 0.97 us -> none  [local(): arrived[:, width].astype(jnp.int32) * 128]
    unnamed x6 -> x12, local copies, waits for them, and re-layouts: 0.01 us -> 0.92 us
where the time goes in v2:
time: 40.6 us; the launch traced here: 40.4 us
  blocking collectives  33.1 us (82%)
  Pallas kernels  5.67 us (14%)
  local copies, waits for them, and re-layouts  0.92 us (2%)
  between operations  0.69 us (2%)
    all_to_all x1, blocking collectives, local(): lax.all_to_all(packed, AXES, split_axis=0, concat_axis=0, tiled=True)  23 us
    all_to_all x1, blocking collectives, local(): heard = lax.all_to_all(told, AXES, split_axis=0, concat_axis=0, tiled=True)  10.1 us
    pallas_call x1, Pallas kernels, local(): pl.pallas_call(functools.partial(advance, block, tile), out_shape=(table,...  3.53 us
    pallas_call x1, Pallas kernels, local(): pl.pallas_call(functools.partial(apply, chunk), out_shape=table, in_specs...  1.94 us
    unnamed x12, local copies, waits for them, and re-layouts  0.92 us

profile of v2, /device:TPU:0, one launch (start us, length us, event | category | flops | bytes accessed | tf_op | source)
XLA Modules:
  0.0 40.4 jit_solution(15757300625317146771)
XLA Ops:
  0.6 0.0 copy-start.4
  0.6 0.0 copy-start.3
  0.7 0.0 copy-start.5
  0.7 0.6 %copy-done.4 = s32[32]{0:T(128)S(1)} copy-done((s32[32]{0:T(128)S(1)}, s32[32]{0:T(128)}, u32[]{:S(2)}) %copy-start.4) | copy-done | bytes 152
  1.3 0.0 copy-done.3
  1.3 0.1 address.1.digits_ref
  1.4 0.3 copy-done.5
  1.7 0.0 copy-start
  1.7 0.0 copy-start.1
  1.7 0.0 copy-start.2
  1.7 0.1 pack.1
  1.8 23.0 %all_to_all.10.arrived_ref = bf16[32,2,4224]{2,1,0:T(2,128)(2,1)S(1)} all-to-all(bf16[32,2,4224]{2,1,0:T(2,128)(2,1)S(1)} %pack.1), channel_id=1, replica_groups=mesh['rows'=8,'dp'=4] {'rows','dp'}, dimensions={0} | all-to-all | bytes 1081344 | tf_op jit(solution)/shard_map/all_to_all | solution.py:162
  24.8 0.0 copy-done
  24.8 0.0 copy-done.1
  24.8 0.0 copy-done.2
  24.8 3.5 %advance.1 = (f32[192,4096]{1,0:T(8,128)}, f32[192,4096]{1,0:T(8,128)}, f32[192,4096]{1,0:T(8,128)S(1)}, f32[32,2,128]{2,1,0:T(2,128)S(1)}) custom-call(bf16[32,2,4224]{2,1,0:T(2,128)(2,1)S(1)} %all_to_all.10.arrived_ref, f32[192,4096]{1,0:T(8,128)S(1)} %copy-done, f32[192,4096]{1,0:T(8,128)S(1)} %copy-done.1, f32[192,4096]{1,0:T(8,128)S(1)} %copy-done.2), custom_call_target="tpu_custom_call" | custom-call | flops 100000000 | tf_op jit(solution)/shard_map/advance/pallas_call | solution.py:163
  28.4 10.1 %all_to_all.11.heard_ref = f32[32,2,128]{2,1,0:T(2,128)S(1)} all-to-all(f32[32,2,128]{2,1,0:T(2,128)S(1)} %get-tuple-element.7), channel_id=1, replica_groups=mesh['rows'=8,'dp'=4] {'rows','dp'}, dimensions={0} | all-to-all | bytes 65536 | tf_op jit(solution)/shard_map/all_to_all | solution.py:179
  38.5 1.9 %apply.1 = f32[192,4096]{1,0:T(8,128)} custom-call(f32[32,2,128]{2,1,0:T(2,128)S(1)} %all_to_all.11.heard_ref, f32[192,4096]{1,0:T(8,128)S(1)} %copy-done, f32[192,4096]{1,0:T(8,128)S(1)} %get-tuple-element.8.update_ref), custom_call_target="tpu_custom_call" | custom-call | flops 1000000 | tf_op jit(solution)/shard_map/apply/pallas_call | solution.py:180
  (1 shorter events, 0.0 us)
Async XLA Ops:
  0.6 0.7 %copy-start.4 = (s32[32]{0:T(128)S(1)}, s32[32]{0:T(128)}, u32[]{:S(2)}) copy-start(s32[32]{0:T(128)} %count_ref.1) | copy-start | bytes 388
  0.6 0.7 %copy-start.3 = (s32[64]{0:T(128)S(1)}, s32[64]{0:T(128)}, u32[]{:S(2)}) copy-start(s32[64]{0:T(128)} %index_ref.1) | copy-start | bytes 772
  0.7 1.1 %copy-start.5 = (bf16[64,4096]{1,0:T(8,128)(2,1)S(1)}, bf16[64,4096]{1,0:T(8,128)(2,1)}, u32[]{:S(2)}) copy-start(bf16[64,4096]{1,0:T(8,128)(2,1)} %tile_ref.1) | copy-start | bytes 1572868
  1.7 23.1 %copy-start = (f32[192,4096]{1,0:T(8,128)S(1)}, f32[192,4096]{1,0:T(8,128)}, u32[]{:S(2)}) copy-start(f32[192,4096]{1,0:T(8,128)} %weights_ref.3) | copy-start | bytes 9437188
  1.7 23.1 %copy-start.1 = (f32[192,4096]{1,0:T(8,128)S(1)}, f32[192,4096]{1,0:T(8,128)}, u32[]{:S(2)}) copy-start(f32[192,4096]{1,0:T(8,128)} %moment_ref.1) | copy-start | bytes 9437188
  1.7 23.1 %copy-start.2 = (f32[192,4096]{1,0:T(8,128)S(1)}, f32[192,4096]{1,0:T(8,128)}, u32[]{:S(2)}) copy-start(f32[192,4096]{1,0:T(8,128)} %second_ref.1) | copy-start | bytes 9437188

commit v3 on v2

--- a/solution.py
+++ b/solution.py
@@ -58,7 +58,7 @@
 
 
 def advance(block, tile, arrived_ref, weights_ref, moment_ref, second_ref,
-            new_moment_hbm, new_second_hbm, update_ref, told_ref,
+            new_moment_hbm, new_second_hbm, late_moment_ref, late_second_ref, update_ref, told_ref,
             new_moment_ref, new_second_ref, even_ref, odd_ref, sem):
     rows_here, width = weights_ref.shape
     owners, capacity, _ = arrived_ref.shape
@@ -84,6 +84,9 @@
         if j + 1 < blocks:
             gather(j + 1, next_ref)
         cols = pl.ds(j * block, block)
+        late = j + 1 == blocks
+        moment_to, second_to = (late_moment_ref, late_second_ref) if late else (new_moment_ref, new_second_ref)
+        into = pl.ds(0, block) if late else cols
         for r in range(0, rows_here, 8):
             rows = pl.ds(r, 8)
             gradient = gradient_ref[rows, :]
@@ -92,11 +95,13 @@
             new_second = beta_two * second_ref[rows, cols] + (1.0 - beta_two) * gradient * gradient
             root = new_second * lax.rsqrt(new_second)
             update = new_moment / (root + epsilon) + decay * weights
-            new_moment_ref[rows, cols] = new_moment
-            new_second_ref[rows, cols] = new_second
+            moment_to[rows, into] = new_moment
+            second_to[rows, into] = new_second
             update_ref[rows, cols] = update
             weight_sum += weights * weights
             update_sum += update * update
+        if late:
+            continue
         for k, (held, out) in enumerate(((new_moment_ref, new_moment_hbm), (new_second_ref, new_second_hbm))):
             stores.append(pltpu.make_async_copy(held.at[:, cols], out.at[:, cols], sem.at[k, j]))
             stores[-1].start()
@@ -111,14 +116,24 @@
         store.wait()
 
 
-def apply(chunk, heard_ref, weights_ref, update_ref, out_ref, held_ref, sem):
+def apply(chunk, heard_ref, weights_ref, update_ref, late_moment_ref, late_second_ref, moment_in, second_in,
+          out_ref, new_moment_hbm, new_second_hbm, held_ref, sem):
+    del moment_in, second_in
+    rows_here, width = weights_ref.shape
+    block = late_moment_ref.shape[1]
+    cols = pl.ds(width - block, block)
+    stores = [
+        pltpu.make_async_copy(late_moment_ref, new_moment_hbm.at[:, cols], sem.at[0]),
+        pltpu.make_async_copy(late_second_ref, new_second_hbm.at[:, cols], sem.at[1]),
+    ]
+    for store in stores:
+        store.start()
     sums = jnp.sum(jnp.sum(heard_ref[...], axis=0), axis=1, keepdims=True)
     scale = rate * (jnp.sqrt(sums[0:1]) / jnp.sqrt(sums[1:2] + 1e-06))
-    stores = []
-    for k in range(weights_ref.shape[0] // chunk):
+    for k in range(rows_here // chunk):
         rows = pl.ds(k * chunk, chunk)
         held_ref[rows, :] = weights_ref[rows, :] - scale * update_ref[rows, :]
-        stores.append(pltpu.make_async_copy(held_ref.at[rows, :], out_ref.at[rows, :], sem.at[k]))
+        stores.append(pltpu.make_async_copy(held_ref.at[rows, :], out_ref.at[rows, :], sem.at[2 + k]))
         stores[-1].start()
     for store in stores:
         store.wait()
@@ -160,11 +175,12 @@
         name="pack",
     )(digits, tile_rows)
     arrived = lax.all_to_all(packed, AXES, split_axis=0, concat_axis=0, tiled=True)
-    new_moment, new_second, update, told = pl.pallas_call(
+    late = jax.ShapeDtypeStruct((rows_here, block), jnp.float32)
+    new_moment, new_second, late_moment, late_second, update, told = pl.pallas_call(
         functools.partial(advance, block, tile),
-        out_shape=(table,) * 3 + (jax.ShapeDtypeStruct((owners, 2, LANES), jnp.float32),),
+        out_shape=(table, table, late, late, table, jax.ShapeDtypeStruct((owners, 2, LANES), jnp.float32)),
         in_specs=[VMEM] * 4,
-        out_specs=(ANY, ANY, VMEM, VMEM),
+        out_specs=(ANY, ANY) + (VMEM,) * 4,
         scratch_shapes=[
             pltpu.VMEM((rows_here, width), jnp.float32),
             pltpu.VMEM((rows_here, width), jnp.float32),
@@ -177,20 +193,20 @@
         name="advance",
     )(arrived, weights, moment, second)
     heard = lax.all_to_all(told, AXES, split_axis=0, concat_axis=0, tiled=True)
-    new_weights = pl.pallas_call(
+    return pl.pallas_call(
         functools.partial(apply, chunk),
-        out_shape=table,
-        in_specs=[VMEM] * 3,
-        out_specs=ANY,
+        out_shape=(table,) * 3,
+        in_specs=[VMEM] * 5 + [ANY] * 2,
+        out_specs=(ANY,) * 3,
+        input_output_aliases={5: 1, 6: 2},
         scratch_shapes=[
             pltpu.VMEM((rows_here, width), jnp.float32),
-            pltpu.SemaphoreType.DMA((rows_here // chunk,)),
+            pltpu.SemaphoreType.DMA((2 + rows_here // chunk,)),
         ],
         compiler_params=pltpu.CompilerParams(vmem_limit_bytes=24 * MIB),
         cost_estimate=cost(1000000),
         name="apply",
-    )(heard, weights, update)
-    return (new_weights, new_moment, new_second)
+    )(heard, weights, update, late_moment, late_second, new_moment, new_second)
 
 
 def solution(mesh):

time: 40.6 us -> 40.4 us (level)
  no operation moved by 1% of the time
where the time goes in v3:
time: 40.4 us; the launch traced here: 40.2 us
  blocking collectives  33.1 us (82%)
  Pallas kernels  5.5 us (14%)
  local copies, waits for them, and re-layouts  0.92 us (2%)
  between operations  0.69 us (2%)
    all_to_all x1, blocking collectives, local(): lax.all_to_all(packed, AXES, split_axis=0, concat_axis=0, tiled=True)  23 us
    all_to_all x1, blocking collectives, local(): heard = lax.all_to_all(told, AXES, split_axis=0, concat_axis=0, tiled=True)  10.1 us
    pallas_call x1, Pallas kernels, local(): pl.pallas_call(functools.partial(advance, block, tile), out_shape=(table,...  3.3 us
    pallas_call x1, Pallas kernels, local(): pl.pallas_call(functools.partial(apply, chunk), out_shape=(table,) * 3, i...  2 us
    unnamed x12, local copies, waits for them, and re-layouts  0.92 us

profile of v3, /device:TPU:0, one launch (start us, length us, event | category | flops | bytes accessed | tf_op | source)
XLA Modules:
  0.0 40.2 jit_solution(15822669215492718584)
XLA Ops:
  0.6 0.0 copy-start.4
  0.6 0.0 copy-start.3
  0.7 0.0 copy-start.5
  0.7 0.6 %copy-done.4 = s32[32]{0:T(128)S(1)} copy-done((s32[32]{0:T(128)S(1)}, s32[32]{0:T(128)}, u32[]{:S(2)}) %copy-start.4) | copy-done | bytes 152
  1.3 0.0 copy-done.3
  1.3 0.1 address.1.digits_ref
  1.4 0.3 copy-done.5
  1.7 0.0 copy-start
  1.7 0.0 copy-start.1
  1.7 0.0 copy-start.2
  1.7 0.1 pack.1
  1.8 23.0 %all_to_all.10.arrived_ref = bf16[32,2,4224]{2,1,0:T(2,128)(2,1)S(1)} all-to-all(bf16[32,2,4224]{2,1,0:T(2,128)(2,1)S(1)} %pack.1), channel_id=1, replica_groups=mesh['rows'=8,'dp'=4] {'rows','dp'}, dimensions={0} | all-to-all | bytes 1081344 | tf_op jit(solution)/shard_map/all_to_all | solution.py:177
  24.8 0.0 copy-done
  24.8 0.0 copy-done.1
  24.8 0.0 copy-done.2
  24.8 3.3 %advance.1 = (f32[192,4096]{1,0:T(8,128)}, f32[192,4096]{1,0:T(8,128)}, f32[192,512]{1,0:T(8,128)S(1)}, f32[192,512]{1,0:T(8,128)S(1)}, f32[192,4096]{1,0:T(8,128)S(1)}, /*index=5*/f32[32,2,128]{2,1,0:T(2,128)S(1)}) custom-call(bf16[32,2,4224]{2,1,0:T(2,128)(2,1)S(1)} %all_to_all.10.arrived_ref, f32[192,4096]{1,0:T(8,128)S(1)} %copy-done, ...), custom_call_target="tpu_custom_call" | custom-call | flops 100000000 | tf_op jit(solution)/shard_map/advance/pallas_call | solution.py:179
  28.1 10.1 %all_to_all.11.heard_ref = f32[32,2,128]{2,1,0:T(2,128)S(1)} all-to-all(f32[32,2,128]{2,1,0:T(2,128)S(1)} %get-tuple-element.9), channel_id=1, replica_groups=mesh['rows'=8,'dp'=4] {'rows','dp'}, dimensions={0} | all-to-all | bytes 65536 | tf_op jit(solution)/shard_map/all_to_all | solution.py:195
  38.2 2.0 %apply.1 = (f32[192,4096]{1,0:T(8,128)}, f32[192,4096]{1,0:T(8,128)}, f32[192,4096]{1,0:T(8,128)}) custom-call(f32[32,2,128]{2,1,0:T(2,128)S(1)} %all_to_all.11.heard_ref, f32[192,4096]{1,0:T(8,128)S(1)} %copy-done, f32[192,4096]{1,0:T(8,128)S(1)} %get-tuple-element.10.update_ref, ...), custom_call_target="tpu_custom_call", output_to_operand_aliasing={{1}: (5, {}), {2}: (6, {})} | custom-call | flops 1000000 | tf_op jit(solution)/shard_map/apply/pallas_call | solution.py:196
  (1 shorter events, 0.0 us)
Async XLA Ops:
  0.6 0.7 %copy-start.4 = (s32[32]{0:T(128)S(1)}, s32[32]{0:T(128)}, u32[]{:S(2)}) copy-start(s32[32]{0:T(128)} %count_ref.1) | copy-start | bytes 388
  0.6 0.7 %copy-start.3 = (s32[64]{0:T(128)S(1)}, s32[64]{0:T(128)}, u32[]{:S(2)}) copy-start(s32[64]{0:T(128)} %index_ref.1) | copy-start | bytes 772
  0.7 1.1 %copy-start.5 = (bf16[64,4096]{1,0:T(8,128)(2,1)S(1)}, bf16[64,4096]{1,0:T(8,128)(2,1)}, u32[]{:S(2)}) copy-start(bf16[64,4096]{1,0:T(8,128)(2,1)} %tile_ref.1) | copy-start | bytes 1572868
  1.7 23.1 %copy-start = (f32[192,4096]{1,0:T(8,128)S(1)}, f32[192,4096]{1,0:T(8,128)}, u32[]{:S(2)}) copy-start(f32[192,4096]{1,0:T(8,128)} %weights_ref.3) | copy-start | bytes 9437188
  1.7 23.1 %copy-start.1 = (f32[192,4096]{1,0:T(8,128)S(1)}, f32[192,4096]{1,0:T(8,128)}, u32[]{:S(2)}) copy-start(f32[192,4096]{1,0:T(8,128)} %moment_ref.1) | copy-start | bytes 9437188
  1.7 23.1 %copy-start.2 = (f32[192,4096]{1,0:T(8,128)S(1)}, f32[192,4096]{1,0:T(8,128)}, u32[]{:S(2)}) copy-start(f32[192,4096]{1,0:T(8,128)} %second_ref.1) | copy-start | bytes 9437188

commit v4 on v3

--- a/solution.py
+++ b/solution.py
@@ -18,7 +18,6 @@
 MIB = 1 << 20
 
 VMEM = pl.BlockSpec(memory_space=pltpu.VMEM)
-SMEM = pl.BlockSpec(memory_space=pltpu.SMEM)
 ANY = pl.BlockSpec(memory_space=pl.ANY)
 
 
@@ -130,9 +129,13 @@
         store.start()
     sums = jnp.sum(jnp.sum(heard_ref[...], axis=0), axis=1, keepdims=True)
     scale = rate * (jnp.sqrt(sums[0:1]) / jnp.sqrt(sums[1:2] + 1e-06))
+    scale = jnp.broadcast_to(scale, (8, block))
     for k in range(rows_here // chunk):
+        for r in range(k * chunk, (k + 1) * chunk, 8):
+            for c in range(0, width, block):
+                here = (pl.ds(r, 8), pl.ds(c, block))
+                held_ref[here] = weights_ref[here] - scale * update_ref[here]
         rows = pl.ds(k * chunk, chunk)
-        held_ref[rows, :] = weights_ref[rows, :] - scale * update_ref[rows, :]
         stores.append(pltpu.make_async_copy(held_ref.at[rows, :], out_ref.at[rows, :], sem.at[2 + k]))
         stores[-1].start()
     for store in stores:
@@ -146,7 +149,8 @@
     capacity = slot_total // owners
     block = math.gcd(width, 512)
     tile = math.gcd(width, 256)
-    chunk = 24
+    chunk = math.gcd(rows_here, 48)
+    assert rows_here % 8 == 0 and rows_here <= 1 << 15
     table = jax.ShapeDtypeStruct((rows_here, width), jnp.float32)
     token = pl.pallas_call(
         start,

time: 40.4 us -> 40.4 us (level)
  no operation moved by 1% of the time
where the time goes in v4:
time: 40.4 us; the launch traced here: 40.2 us
  blocking collectives  33.1 us (82%)
  Pallas kernels  5.47 us (14%)
  local copies, waits for them, and re-layouts  0.92 us (2%)
  between operations  0.69 us (2%)
    all_to_all x1, blocking collectives, local(): lax.all_to_all(packed, AXES, split_axis=0, concat_axis=0, tiled=True)  23 us
    all_to_all x1, blocking collectives, local(): heard = lax.all_to_all(told, AXES, split_axis=0, concat_axis=0, tiled=True)  10.1 us
    pallas_call x1, Pallas kernels, local(): pl.pallas_call(functools.partial(advance, block, tile), out_shape=(table,...  3.3 us
    pallas_call x1, Pallas kernels, local(): pl.pallas_call(functools.partial(apply, chunk), out_shape=(table,) * 3, i...  1.97 us
    unnamed x12, local copies, waits for them, and re-layouts  0.92 us

profile of v4, /device:TPU:0, one launch (start us, length us, event | category | flops | bytes accessed | tf_op | source)
XLA Modules:
  0.0 40.2 jit_solution(8456875635004142282)
XLA Ops:
  0.6 0.0 copy-start.4
  0.6 0.0 copy-start.3
  0.7 0.0 copy-start.5
  0.7 0.6 %copy-done.4 = s32[32]{0:T(128)S(1)} copy-done((s32[32]{0:T(128)S(1)}, s32[32]{0:T(128)}, u32[]{:S(2)}) %copy-start.4) | copy-done | bytes 152
  1.3 0.0 copy-done.3
  1.3 0.1 address.1.digits_ref
  1.4 0.3 copy-done.5
  1.7 0.0 copy-start
  1.7 0.0 copy-start.1
  1.7 0.0 copy-start.2
  1.7 0.1 pack.1
  1.8 23.0 %all_to_all.10.arrived_ref = bf16[32,2,4224]{2,1,0:T(2,128)(2,1)S(1)} all-to-all(bf16[32,2,4224]{2,1,0:T(2,128)(2,1)S(1)} %pack.1), channel_id=1, replica_groups=mesh['rows'=8,'dp'=4] {'rows','dp'}, dimensions={0} | all-to-all | bytes 1081344 | tf_op jit(solution)/shard_map/all_to_all | solution.py:181
  24.8 0.0 copy-done
  24.8 0.0 copy-done.1
  24.8 0.0 copy-done.2
  24.8 3.3 %advance.1 = (f32[192,4096]{1,0:T(8,128)}, f32[192,4096]{1,0:T(8,128)}, f32[192,512]{1,0:T(8,128)S(1)}, f32[192,512]{1,0:T(8,128)S(1)}, f32[192,4096]{1,0:T(8,128)S(1)}, /*index=5*/f32[32,2,128]{2,1,0:T(2,128)S(1)}) custom-call(bf16[32,2,4224]{2,1,0:T(2,128)(2,1)S(1)} %all_to_all.10.arrived_ref, f32[192,4096]{1,0:T(8,128)S(1)} %copy-done, ...), custom_call_target="tpu_custom_call" | custom-call | flops 100000000 | tf_op jit(solution)/shard_map/advance/pallas_call | solution.py:183
  28.1 10.1 %all_to_all.11.heard_ref = f32[32,2,128]{2,1,0:T(2,128)S(1)} all-to-all(f32[32,2,128]{2,1,0:T(2,128)S(1)} %get-tuple-element.9), channel_id=1, replica_groups=mesh['rows'=8,'dp'=4] {'rows','dp'}, dimensions={0} | all-to-all | bytes 65536 | tf_op jit(solution)/shard_map/all_to_all | solution.py:199
  38.2 2.0 %apply.1 = (f32[192,4096]{1,0:T(8,128)}, f32[192,4096]{1,0:T(8,128)}, f32[192,4096]{1,0:T(8,128)}) custom-call(f32[32,2,128]{2,1,0:T(2,128)S(1)} %all_to_all.11.heard_ref, f32[192,4096]{1,0:T(8,128)S(1)} %copy-done, f32[192,4096]{1,0:T(8,128)S(1)} %get-tuple-element.10.update_ref, ...), custom_call_target="tpu_custom_call", output_to_operand_aliasing={{1}: (5, {}), {2}: (6, {})} | custom-call | flops 1000000 | tf_op jit(solution)/shard_map/apply/pallas_call | solution.py:200
  (1 shorter events, 0.0 us)
Async XLA Ops:
  0.6 0.7 %copy-start.4 = (s32[32]{0:T(128)S(1)}, s32[32]{0:T(128)}, u32[]{:S(2)}) copy-start(s32[32]{0:T(128)} %count_ref.1) | copy-start | bytes 388
  0.6 0.7 %copy-start.3 = (s32[64]{0:T(128)S(1)}, s32[64]{0:T(128)}, u32[]{:S(2)}) copy-start(s32[64]{0:T(128)} %index_ref.1) | copy-start | bytes 772
  0.7 1.1 %copy-start.5 = (bf16[64,4096]{1,0:T(8,128)(2,1)S(1)}, bf16[64,4096]{1,0:T(8,128)(2,1)}, u32[]{:S(2)}) copy-start(bf16[64,4096]{1,0:T(8,128)(2,1)} %tile_ref.1) | copy-start | bytes 1572868
  1.7 23.1 %copy-start = (f32[192,4096]{1,0:T(8,128)S(1)}, f32[192,4096]{1,0:T(8,128)}, u32[]{:S(2)}) copy-start(f32[192,4096]{1,0:T(8,128)} %weights_ref.3) | copy-start | bytes 9437188
  1.7 23.1 %copy-start.1 = (f32[192,4096]{1,0:T(8,128)S(1)}, f32[192,4096]{1,0:T(8,128)}, u32[]{:S(2)}) copy-start(f32[192,4096]{1,0:T(8,128)} %moment_ref.1) | copy-start | bytes 9437188
  1.7 23.1 %copy-start.2 = (f32[192,4096]{1,0:T(8,128)S(1)}, f32[192,4096]{1,0:T(8,128)}, u32[]{:S(2)}) copy-start(f32[192,4096]{1,0:T(8,128)} %second_ref.1) | copy-start | bytes 9437188

commit v5 on v4

--- a/solution.py
+++ b/solution.py
@@ -1,4 +1,5 @@
 import functools
+import itertools
 import math
 
 import jax
@@ -74,8 +75,8 @@
             sent = arrived_ref[:, :, j * block + k:j * block + k + tile].reshape(slots, tile)
             gradient_ref[:, k:k + tile] = jnp.dot(picker, sent, preferred_element_type=jnp.float32)
 
-    weight_sum = jnp.zeros((8, block), jnp.float32)
-    update_sum = jnp.zeros((8, block), jnp.float32)
+    weight_sum = jnp.zeros((8, tile), jnp.float32)
+    update_sum = jnp.zeros((8, tile), jnp.float32)
     stores = []
     gather(0, even_ref)
     for j in range(blocks):
@@ -85,18 +86,18 @@
         cols = pl.ds(j * block, block)
         late = j + 1 == blocks
         moment_to, second_to = (late_moment_ref, late_second_ref) if late else (new_moment_ref, new_second_ref)
-        into = pl.ds(0, block) if late else cols
-        for r in range(0, rows_here, 8):
-            rows = pl.ds(r, 8)
-            gradient = gradient_ref[rows, :]
-            weights = weights_ref[rows, cols]
-            new_moment = beta_one * moment_ref[rows, cols] + (1.0 - beta_one) * gradient
-            new_second = beta_two * second_ref[rows, cols] + (1.0 - beta_two) * gradient * gradient
+        for r, c in itertools.product(range(0, rows_here, 8), range(0, block, tile)):
+            rows, some = pl.ds(r, 8), pl.ds(j * block + c, tile)
+            into = pl.ds(c, tile) if late else some
+            gradient = gradient_ref[rows, pl.ds(c, tile)]
+            weights = weights_ref[rows, some]
+            new_moment = beta_one * moment_ref[rows, some] + (1.0 - beta_one) * gradient
+            new_second = beta_two * second_ref[rows, some] + (1.0 - beta_two) * gradient * gradient
             root = new_second * lax.rsqrt(new_second)
             update = new_moment / (root + epsilon) + decay * weights
             moment_to[rows, into] = new_moment
             second_to[rows, into] = new_second
-            update_ref[rows, cols] = update
+            update_ref[rows, some] = update
             weight_sum += weights * weights
             update_sum += update * update
         if late:
@@ -107,7 +108,7 @@
 
     def narrow(x):
         x = jnp.sum(x, axis=0, keepdims=True)
-        return sum(x[:, k:k + LANES] for k in range(0, block, LANES))
+        return sum(x[:, k:k + LANES] for k in range(0, tile, LANES))
 
     both = jnp.concatenate([narrow(weight_sum), narrow(update_sum)], axis=0)
     told_ref[...] = jnp.broadcast_to(both[None], told_ref.shape)

time: 40.4 us -> 40.4 us (level)
  no operation moved by 1% of the time
where the time goes in v5:
time: 40.4 us; the launch traced here: 40.2 us
  blocking collectives  33.1 us (82%)
  Pallas kernels  5.43 us (13%)
  local copies, waits for them, and re-layouts  0.92 us (2%)
  between operations  0.69 us (2%)
    all_to_all x1, blocking collectives, local(): lax.all_to_all(packed, AXES, split_axis=0, concat_axis=0, tiled=True)  23 us
    all_to_all x1, blocking collectives, local(): heard = lax.all_to_all(told, AXES, split_axis=0, concat_axis=0, tiled=True)  10.1 us
    pallas_call x1, Pallas kernels, local(): pl.pallas_call(functools.partial(advance, block, tile), out_shape=(table,...  3.26 us
    pallas_call x1, Pallas kernels, local(): pl.pallas_call(functools.partial(apply, chunk), out_shape=(table,) * 3, i...  1.97 us
    unnamed x12, local copies, waits for them, and re-layouts  0.92 us

profile of v5, /device:TPU:0, one launch (start us, length us, event | category | flops | bytes accessed | tf_op | source)
XLA Modules:
  0.0 40.2 jit_solution(2161120915570713915)
XLA Ops:
  0.6 0.0 copy-start.4
  0.6 0.0 copy-start.3
  0.7 0.0 copy-start.5
  0.7 0.6 %copy-done.4 = s32[32]{0:T(128)S(1)} copy-done((s32[32]{0:T(128)S(1)}, s32[32]{0:T(128)}, u32[]{:S(2)}) %copy-start.4) | copy-done | bytes 152
  1.3 0.0 copy-done.3
  1.3 0.1 address.1.digits_ref
  1.4 0.3 copy-done.5
  1.7 0.0 copy-start
  1.7 0.0 copy-start.1
  1.7 0.0 copy-start.2
  1.7 0.1 pack.1
  1.8 23.0 %all_to_all.10.arrived_ref = bf16[32,2,4224]{2,1,0:T(2,128)(2,1)S(1)} all-to-all(bf16[32,2,4224]{2,1,0:T(2,128)(2,1)S(1)} %pack.1), channel_id=1, replica_groups=mesh['rows'=8,'dp'=4] {'rows','dp'}, dimensions={0} | all-to-all | bytes 1081344 | tf_op jit(solution)/shard_map/all_to_all | solution.py:182
  24.8 0.0 copy-done
  24.8 0.0 copy-done.1
  24.8 0.0 copy-done.2
  24.8 3.3 %advance.1 = (f32[192,4096]{1,0:T(8,128)}, f32[192,4096]{1,0:T(8,128)}, f32[192,512]{1,0:T(8,128)S(1)}, f32[192,512]{1,0:T(8,128)S(1)}, f32[192,4096]{1,0:T(8,128)S(1)}, /*index=5*/f32[32,2,128]{2,1,0:T(2,128)S(1)}) custom-call(bf16[32,2,4224]{2,1,0:T(2,128)(2,1)S(1)} %all_to_all.10.arrived_ref, f32[192,4096]{1,0:T(8,128)S(1)} %copy-done, ...), custom_call_target="tpu_custom_call" | custom-call | flops 100000000 | tf_op jit(solution)/shard_map/advance/pallas_call | solution.py:184
  28.1 10.1 %all_to_all.11.heard_ref = f32[32,2,128]{2,1,0:T(2,128)S(1)} all-to-all(f32[32,2,128]{2,1,0:T(2,128)S(1)} %get-tuple-element.9), channel_id=1, replica_groups=mesh['rows'=8,'dp'=4] {'rows','dp'}, dimensions={0} | all-to-all | bytes 65536 | tf_op jit(solution)/shard_map/all_to_all | solution.py:200
  38.2 2.0 %apply.1 = (f32[192,4096]{1,0:T(8,128)}, f32[192,4096]{1,0:T(8,128)}, f32[192,4096]{1,0:T(8,128)}) custom-call(f32[32,2,128]{2,1,0:T(2,128)S(1)} %all_to_all.11.heard_ref, f32[192,4096]{1,0:T(8,128)S(1)} %copy-done, f32[192,4096]{1,0:T(8,128)S(1)} %get-tuple-element.10.update_ref, ...), custom_call_target="tpu_custom_call", output_to_operand_aliasing={{1}: (5, {}), {2}: (6, {})} | custom-call | flops 1000000 | tf_op jit(solution)/shard_map/apply/pallas_call | solution.py:201
  (1 shorter events, 0.0 us)
Async XLA Ops:
  0.6 0.7 %copy-start.4 = (s32[32]{0:T(128)S(1)}, s32[32]{0:T(128)}, u32[]{:S(2)}) copy-start(s32[32]{0:T(128)} %count_ref.1) | copy-start | bytes 388
  0.6 0.7 %copy-start.3 = (s32[64]{0:T(128)S(1)}, s32[64]{0:T(128)}, u32[]{:S(2)}) copy-start(s32[64]{0:T(128)} %index_ref.1) | copy-start | bytes 772
  0.7 1.1 %copy-start.5 = (bf16[64,4096]{1,0:T(8,128)(2,1)S(1)}, bf16[64,4096]{1,0:T(8,128)(2,1)}, u32[]{:S(2)}) copy-start(bf16[64,4096]{1,0:T(8,128)(2,1)} %tile_ref.1) | copy-start | bytes 1572868
  1.7 23.1 %copy-start = (f32[192,4096]{1,0:T(8,128)S(1)}, f32[192,4096]{1,0:T(8,128)}, u32[]{:S(2)}) copy-start(f32[192,4096]{1,0:T(8,128)} %weights_ref.3) | copy-start | bytes 9437188
  1.7 23.1 %copy-start.1 = (f32[192,4096]{1,0:T(8,128)S(1)}, f32[192,4096]{1,0:T(8,128)}, u32[]{:S(2)}) copy-start(f32[192,4096]{1,0:T(8,128)} %moment_ref.1) | copy-start | bytes 9437188
  1.7 23.1 %copy-start.2 = (f32[192,4096]{1,0:T(8,128)S(1)}, f32[192,4096]{1,0:T(8,128)}, u32[]{:S(2)}) copy-start(f32[192,4096]{1,0:T(8,128)} %second_ref.1) | copy-start | bytes 9437188
